TPU v7x, 32 devices: a whole 2x2x4 slice. The times are simulated.
32 devices in a mesh: dp: 8 (over z, y), mp: 4 (over x, core).
Axes of the slice: x: 2, y: 2, z: 4, core: 2. Of those that a mesh axis runs over, the one named last changes fastest.
Arguments:
- grads: bfloat16 [8, 8, 128, 128], P('dp', None, 'mp'), may hold values from -24 to 24
- weights: bfloat16 [8, 128, 128], P(None, 'mp'), may hold values from -0.5 to 0.5
- moment1: float32 [16, 128, 128], P('dp', 'mp'), may hold values from -6 to 6
- moment2: float32 [16, 128, 128], P('dp', 'mp'), may hold values from 0.25 to 4
- slot_of_block: int32 [8], replicated, may hold values from 0 to 15, as said below
- trainable: int32 [8], replicated, may hold values 0 or 1
- width_of_block: int32 [8], replicated, may hold values from 64 to 128
Outputs:
- moment1_new: float32 [16, 128, 128], P('dp', 'mp')
- moment2_new: float32 [16, 128, 128], P('dp', 'mp')
- weights_new: bfloat16 [8, 128, 128], P(None, 'mp')
- grad_rms: float32 [], replicated
Inputs may be any that keep to these rules, and one draw needn't show every extreme that they name: `slot_of_block`: all values differ; slot s belongs to owner s // 2 of dp; every owner holds at most 2 blocks and some owner exactly 2.
All inputs are finite; a program needn't handle non-finite values.
Results may differ from a plain program's by a relative error of at most 0.001.
Values may be sent and summed in bfloat16 or wider, within the bound.
No kernel may reach another device: no remote copies, remote signals or barrier semaphores. Data moves between devices by JAX's collectives and lax.ppermute only.
A program may use at most 64 MiB of HBM per device.

v0:
```python
import jax
import jax.numpy as jnp
from jax import lax
from jax.sharding import PartitionSpec as P

STEP = 20


def local(grads, weights, moment1, moment2, slot_of_block, trainable, width_of_block):
    blocks = weights.shape[0]
    row_share = weights.shape[1]
    block_size = weights.shape[2]
    capacity = moment1.shape[0]
    local_grads = grads[0].reshape(blocks, row_share * block_size)
    owner_index = lax.axis_index("dp")
    own_slots = owner_index * capacity + jnp.arange(capacity, dtype=jnp.int32)
    owned_onehot = slot_of_block[None, :] == own_slots[:, None]
    columns = jnp.arange(block_size, dtype=jnp.int32)
    live = ((trainable[:, None] > 0) & (columns[None, :] < width_of_block[:, None])).astype(
        jnp.float32
    )
    slot_live = jnp.dot(owned_onehot.astype(jnp.float32), live, precision=lax.Precision.HIGHEST)
    count = jnp.sum(live) * block_size
    summed = lax.psum(local_grads.astype(jnp.float32), "dp")
    summed_blocks = summed.reshape(blocks, row_share, block_size)
    partial_sq = jnp.sum(summed_blocks * summed_blocks * live[:, None, :])
    sumsq = lax.psum(partial_sq, "mp")
    slot_grad = jnp.dot(
        owned_onehot.astype(jnp.float32), summed, precision=lax.Precision.HIGHEST
    ).reshape(capacity, row_share, block_size)
    grad_rms = jnp.sqrt(sumsq) / jnp.sqrt(jnp.maximum(count, 1.0))
    clip = 1.0 / jnp.maximum(grad_rms, 1.0)
    update_mask = slot_live[:, None, :] > 0
    clipped = clip * slot_grad
    first_new = jnp.where(update_mask, 0.9 * moment1 + 0.1 * clipped, moment1)
    second_new = jnp.where(update_mask, 0.95 * moment2 + 0.05 * clipped * clipped, moment2)
    direction = first_new / (1.0 - 0.9**STEP) / (jnp.sqrt(second_new / (1.0 - 0.95**STEP)) + 1e-08)
    slot_weight = jnp.dot(
        owned_onehot.astype(jnp.bfloat16),
        weights.reshape(blocks, row_share * block_size),
        preferred_element_type=jnp.float32,
    ).reshape(capacity, row_share, block_size)
    slot_new = jnp.where(
        update_mask, slot_weight - 0.001 * (direction + 0.1 * slot_weight), slot_weight
    )
    slot_new = slot_new.astype(jnp.bfloat16).reshape(capacity, row_share * block_size)
    every_slot = lax.all_gather(slot_new, "dp", axis=0, tiled=True)
    slot_total = every_slot.shape[0]
    placing = (slot_of_block[:, None] == jnp.arange(slot_total, dtype=jnp.int32)[None, :]).astype(
        jnp.bfloat16
    )
    weights_new = jnp.dot(placing, every_slot, preferred_element_type=jnp.float32).astype(
        jnp.bfloat16
    )
    return (first_new, second_new, weights_new.reshape(blocks, row_share, block_size), grad_rms)


def solution(mesh):
    return jax.shard_map(
        local,
        mesh=mesh,
        in_specs=(
            P("dp", None, "mp", None),
            P(None, "mp", None),
            P("dp", "mp", None),
            P("dp", "mp", None),
            P(),
            P(),
            P(),
        ),
        out_specs=(P("dp", "mp", None), P("dp", "mp", None), P(None, "mp", None), P()),
        check_vma=False,
    )
```

profile of v0, /device:TPU:0, one launch (start us, length us, event | category | flops | bytes accessed | tf_op | source)
XLA Modules:
  0.0 134.0 jit_solution(4981722641501914412)
XLA Ops:
  7.2 0.0 all-reduce.2.cloned.1.call-start
  7.2 0.9 convert_bitcast_fusion
  8.1 0.7 copy.48
  8.8 0.0 copy-start.1
  8.8 0.0 all-reduce.2.cloned.1.call-update
  8.8 0.0 copy-start.6
  8.8 0.7 copy-done.6
  9.5 0.0 copy-start.5
  9.5 0.6 copy-done.5
  10.2 0.7 fusion.18
  10.8 0.1 fusion.11
  11.6 0.0 copy-start.4
  11.6 0.0 copy-done.1
  11.6 0.6 copy-done.4
  12.2 0.2 fusion.3
  12.4 0.2 convolution_compare_fusion
  12.6 71.8 %all-reduce.2.cloned.1.call-done = f32[8,4096]{1,0:T(8,128)} async-done(((f32[8,4096]{1,0:T(8,128)}), f32[8,4096]{1,0:T(8,128)}) %all-reduce.2.cloned.1.call-update) | async-done | bytes 131088 | tf_op jit(solution)/shard_map/psum | solution.py:24
  84.4 0.0 copy-start
  84.4 1.6 %fusion.2 = f32[]{:T(128)} fusion(f32[8,4096]{1,0:T(8,128)} %all-reduce.2.cloned.1.call-done, f32[8,128]{1,0:T(8,128)S(1)} %fusion.11), kind=kLoop, calls=%fused_computation.7 | loop fusion | flops 98303 | bytes 135172 | tf_op jit(solution)/shard_map/reduce_sum | solution.py:26
  86.1 6.3 %psum.15 = f32[]{:T(128)} all-reduce(f32[]{:T(128)} %fusion.2), channel_id=1, replica_groups=mesh['dp'=8,'mp'=4] {'mp'}, use_global_device_ids=true, to_apply=%region_2.0 | all-reduce | flops 1 | bytes 8 | tf_op jit(solution)/shard_map/psum | solution.py:27
  93.2 0.0 copy-done
  93.2 0.0 copy-start.2
  93.2 0.0 copy-start.3
  93.2 0.3 fusion.1
  93.4 0.5 copy-done.2
  93.9 0.0 copy-done.3
  93.9 0.6 fusion.7
  94.6 30.5 %all-gather = bf16[8,2,4096]{2,1,0:T(2,128)(2,1)S(1)} all-gather(bf16[1,2,4096]{2,1,0:T(2,128)(2,1)S(1)} %reshape.67), channel_id=1, replica_groups=mesh['dp'=8,'mp'=4] {'dp'}, dimensions={0}, use_global_device_ids=true | all-gather | bytes 147456 | tf_op jit(solution)/shard_map/all_gather | solution.py:47
  125.1 0.1 reshape.68
  125.2 0.2 fusion
  125.4 0.6 copy.34
  (3 shorter events, 0.0 us)
Async XLA Ops:
  7.2 77.3 %all-reduce.2.cloned.1.call-start = ((), (), s32[]{:S(2)}) async-start(), calls=%async_computation | async-start | bytes 262144 | tf_op jit(solution)/shard_map/psum | solution.py:24
  8.8 2.8 %copy-start.1 = (bf16[8,32,128]{2,1,0:T(8,128)(2,1)S(1)}, bf16[8,32,128]{2,1,0:T(8,128)(2,1)}, u32[]{:S(2)}) copy-start(bf16[8,32,128]{2,1,0:T(8,128)(2,1)} %param.8) | copy-start | bytes 196612
  8.8 0.7 copy-start.6
  9.5 0.7 copy-start.5
  11.6 0.7 copy-start.4
  84.4 8.7 %copy-start = (f32[8,4096]{1,0:T(8,128)S(1)}, f32[8,4096]{1,0:T(8,128)}, u32[]{:S(2)}) copy-start(f32[8,4096]{1,0:T(8,128)} %all-reduce.2.cloned.1.call-done) | copy-start | bytes 393220
  93.2 0.8 copy-start.2
  93.2 0.8 copy-start.3
Sparse Core Ops, SparseCore 0:
  11.3 73.0 all-reduce.1
where the time goes:
time: 134 us
  waiting for transfers between devices  71.8 us (54%)
  blocking collectives  36.8 us (27%)
  between operations  16.7 us (12%)
  local copies, waits for them, and re-layouts  3.92 us (3%)
  other arithmetic  3.86 us (3%)
    psum x1, waiting for transfers between devices, local(): summed = lax.psum(local_grads.astype(jnp.float32), 'dp')  71.8 us
    all_gather x1, blocking collectives, local(): every_slot = lax.all_gather(slot_new, 'dp', axis=0, tiled=True)  30.5 us
    psum x1, blocking collectives, local(): sumsq = lax.psum(partial_sq, 'mp')  6.3 us
    unnamed x18, local copies, waits for them, and re-layouts  3.92 us
  transfers between devices with their start and end apart: 1, of which 1 were waited for; matrix products, arithmetic and copies ran while one was open for 1% of the time, Pallas kernels for 0%

commit v1 on v0

--- a/solution.py
+++ b/solution.py
@@ -21,7 +21,7 @@
     )
     slot_live = jnp.dot(owned_onehot.astype(jnp.float32), live, precision=lax.Precision.HIGHEST)
     count = jnp.sum(live) * block_size
-    summed = lax.psum(local_grads.astype(jnp.float32), "dp")
+    summed = jnp.sum(lax.all_gather(local_grads.astype(jnp.float32), "dp"), axis=0)
     summed_blocks = summed.reshape(blocks, row_share, block_size)
     partial_sq = jnp.sum(summed_blocks * summed_blocks * live[:, None, :])
     sumsq = lax.psum(partial_sq, "mp")

time: 134 us -> 104 us (0.78)
  waiting for transfers between devices: 71.8 us -> 40.8 us
  local copies, waits for them, and re-layouts: 3.92 us -> 5.41 us
    psum x1 -> x0, waiting for transfers between devices: 71.8 us -> none  [local(): summed = lax.psum(local_grads.astype(jnp.float32), 'dp')]
    all_gather x0 -> x1, waiting for transfers between devices: none -> 40.8 us  [local(): lax.all_gather(local_grads.astype(jnp.float32), 'dp')]
    convert_element_type x0 -> x1, local copies, waits for them, and re-layouts: none -> 1.52 us  [local(): local_grads.astype(jnp.float32)]
    unnamed x18 -> x16, local copies, waits for them, and re-layouts: 3.92 us -> 3.89 us
where the time goes in v1:
time: 104 us; the launch traced here: 103 us
  waiting for transfers between devices  40.8 us (39%)
  blocking collectives  36.8 us (35%)
  between operations  16.7 us (16%)
  local copies, waits for them, and re-layouts  5.41 us (5%)
  other arithmetic  2.67 us (3%)
    all_gather x1, waiting for transfers between devices, local(): lax.all_gather(local_grads.astype(jnp.float32), 'dp')  40.8 us
    all_gather x1, blocking collectives, local(): every_slot = lax.all_gather(slot_new, 'dp', axis=0, tiled=True)  30.5 us
    psum x1, blocking collectives, local(): sumsq = lax.psum(partial_sq, 'mp')  6.3 us
    unnamed x16, local copies, waits for them, and re-layouts  3.89 us
  transfers between devices with their start and end apart: 1, of which 1 were waited for; matrix products, arithmetic and copies ran while one was open for 1% of the time, Pallas kernels for 0%

profile of v1, /device:TPU:0, one launch (start us, length us, event | category | flops | bytes accessed | tf_op | source)
XLA Modules:
  0.0 103.4 jit_solution(13501798082361253344)
XLA Ops:
  7.2 0.0 all-gather.3.cloned.1.call-start
  7.2 1.5 %reshape.79 = f32[1,8,4096]{2,1,0:T(8,128)} reshape(bf16[1,8,32,128]{3,2,1,0:T(8,128)(2,1)} %param.7) | data formatting | bytes 196608 | tf_op jit(solution)/shard_map/convert_element_type | solution.py:24
  8.7 0.0 all-gather.3.cloned.1.call-update
  8.8 0.0 copy-start.5
  8.8 0.6 copy-done.5
  9.4 0.0 copy-start.1
  9.4 0.6 copy-done.1
  10.1 0.7 fusion.16
  11.4 0.0 copy-start
  11.4 0.6 copy-done
  12.1 0.2 convolution_compare_fusion
  12.2 0.1 fusion.10
  12.3 40.8 %all-gather.3.cloned.1.call-done = f32[8,8,4096]{2,1,0:T(8,128)} async-done(((f32[1,8,4096]{2,1,0:T(8,128)}), f32[8,8,4096]{2,1,0:T(8,128)}) %all-gather.3.cloned.1.call-update) | async-done | bytes 1048592 | tf_op jit(solution)/shard_map/all_gather | solution.py:24
  53.1 1.3 %reduce_sum.27 = f32[8,4096]{1,0:T(8,128)S(1)} reduce(f32[8,8,4096]{2,1,0:T(8,128)} %all-gather.3.cloned.1.call-done, f32[]{:T(128)} %constant.7.clone.1), dimensions={0}, to_apply=%region_0.0 | reduce | flops 229376 | bytes 1179652 | tf_op jit(solution)/shard_map/reduce_sum | solution.py:24
  54.4 0.0 copy-start.3
  54.4 0.0 copy-start.4
  54.5 0.6 fusion.2
  55.1 6.3 %psum.7 = f32[]{:T(128)} all-reduce(f32[]{:T(128)} %fusion.2), channel_id=1, replica_groups=mesh['dp'=8,'mp'=4] {'mp'}, use_global_device_ids=true, to_apply=%region_2.0 | all-reduce | flops 1 | bytes 8 | tf_op jit(solution)/shard_map/psum | solution.py:27
  62.2 0.0 copy-done.3
  62.2 0.0 copy-done.4
  62.2 0.3 fusion.6
  62.5 0.0 copy-start.2
  62.5 0.6 copy.29
  63.1 0.6 copy.30
  63.7 0.0 copy-done.2
  63.7 0.2 fusion.8
  64.0 30.5 %all-gather = bf16[8,2,4096]{2,1,0:T(2,128)(2,1)S(1)} all-gather(bf16[1,2,4096]{2,1,0:T(2,128)(2,1)S(1)} %fusion.8), channel_id=1, replica_groups=mesh['dp'=8,'mp'=4] {'dp'}, dimensions={0}, use_global_device_ids=true | all-gather | bytes 147456 | tf_op jit(solution)/shard_map/all_gather | solution.py:47
  94.5 0.1 reshape.81
  94.6 0.2 fusion
  94.8 0.6 copy.31
  (2 shorter events, 0.0 us)
Async XLA Ops:
  7.2 46.0 %all-gather.3.cloned.1.call-start = ((), (), s32[]{:S(2)}) async-start(), calls=%async_computation | async-start | bytes 1179648 | tf_op jit(solution)/shard_map/all_gather | solution.py:24
  8.8 0.7 copy-start.5
  9.4 0.7 copy-start.1
  11.4 0.7 copy-start
  54.4 7.7 %copy-start.3 = (f32[2,32,128]{2,1,0:T(8,128)S(1)}, f32[2,32,128]{2,1,0:T(8,128)}, u32[]{:S(2)}) copy-start(f32[2,32,128]{2,1,0:T(8,128)} %param.10) | copy-start | bytes 98308
  54.4 7.7 %copy-start.4 = (f32[2,32,128]{2,1,0:T(8,128)S(1)}, f32[2,32,128]{2,1,0:T(8,128)}, u32[]{:S(2)}) copy-start(f32[2,32,128]{2,1,0:T(8,128)} %param.9) | copy-start | bytes 98308
  62.5 1.2 %copy-start.2 = (bf16[8,32,128]{2,1,0:T(8,128)(2,1)S(1)}, bf16[8,32,128]{2,1,0:T(8,128)(2,1)}, u32[]{:S(2)}) copy-start(bf16[8,32,128]{2,1,0:T(8,128)(2,1)} %param.8) | copy-start | bytes 196612
Sparse Core Ops, SparseCore 0:
  10.1 42.9 all-gather.2
